TPU v7x, 512 devices: a 8x2x16 block of a 8x8x16 slice. The times are simulated.
512 devices in a mesh: groups: 2 (over y), ctx: 16 (over z), seq: 8 (over x), head: 2 (over core).
Axes of the slice: x: 8, y: 2, z: 16, core: 2. Of those that a mesh axis runs over, the one named last changes fastest.
The devices are a block of a 8x8x16 slice.
Arguments:
- queries: bfloat16 [16, 4, 128, 576], P(('groups', 'seq'), None, ('ctx', 'head')), parts along dimension 0, may hold values from -36 to 36
- cache: bfloat16 [16, 49152, 576], P(('groups', 'seq'), 'ctx'), parts along dimension 0, may hold values from -8 to 8
- lengths: int32 [16], P(('groups', 'seq')), parts along dimension 0, may hold values from 12288 to 49152, as said below
- offsets: int32 [16, 4], P(('groups', 'seq')), parts along dimension 0, may hold values from 0 to 3
- w_uv: bfloat16 [128, 512, 128], P(('ctx', 'head')), may hold values from -0.25 to 0.25
- w_out: bfloat16 [16384, 7168], P(('ctx', 'head'), 'seq'), may hold values from -0.046875 to 0.046875
Outputs:
- mixed: bfloat16 [64, 7168], P(('groups', 'ctx', 'head'), 'seq'), parts along dimension 0
There are 2 independent parts, one for each index of `groups`. A program takes and returns all parts, laid end to end along the dimension named above; an argument that names none is the same for every part. Nothing has to cross between parts.
Inputs may be any that keep to these rules, and one draw needn't show every extreme that they name: `lengths`: each sequence's filled length, its 4 draft tokens included; some sequence reaches 49152 in every draw. Draft token t of sequence s sits at position lengths[s] - 4 + offsets[s, t].
All inputs are finite; a program needn't handle non-finite values.
Results may differ from a plain program's by a relative error of at most 0.014.
Values may be sent and summed in bfloat16 or wider, within the bound.
No kernel may reach another device: no remote copies, remote signals or barrier semaphores. Data moves between devices by JAX's collectives and lax.ppermute only.
A program may use at most 64 MiB of HBM per device.

v0:
```python
import math

import jax
import jax.numpy as jnp
from jax import lax
from jax.sharding import PartitionSpec as P

LATENT = 512
ROPE = 64
NOPE = 128
DRAFT = 4


theta = 10000.0
negative = -1e30


def copy_for_each(value, axis):
    devices = lax.axis_size(axis)
    return lax.all_to_all(
        jnp.broadcast_to(value[None], (devices, *value.shape)), axis, 0, 0, tiled=True
    )


def taken_together(value, axis):
    return copy_for_each(value, axis).max(axis=0)


def cut_along(value, dim, devices):
    dims = value.shape
    blocks = value.reshape(*dims[:dim], devices, dims[dim] // devices, *dims[dim + 1 :])
    return jnp.moveaxis(blocks, dim, 0)


def sent_and_summed(value, axis, dim):
    blocks = cut_along(value, dim, lax.axis_size(axis))
    arrived = lax.all_to_all(blocks, axis, split_axis=0, concat_axis=0, tiled=True)
    return arrived.sum(axis=0)


def sent_together(arrays, axis, dim, along):
    widths = [math.prod(a.shape[along:]) for a in arrays]
    both = jnp.concatenate(
        [a.reshape(*a.shape[:along], w) for a, w in zip(arrays, widths)], axis=along
    )
    result = sent_and_summed(both, axis, dim)
    blocks = jnp.split(result, [sum(widths[:k]) for k in range(1, len(widths))], axis=along)
    return tuple(
        (b.reshape(*result.shape[:along], *a.shape[along:]) for a, b in zip(arrays, blocks))
    )


def joined_along(blocks, dim):
    blocks = jnp.moveaxis(blocks, 0, dim)
    dims = blocks.shape
    return blocks.reshape(*dims[:dim], dims[dim] * dims[dim + 1], *dims[dim + 2 :])


def collect(value, axis, dim):
    return joined_along(copy_for_each(value, axis), dim)


def rotate(queries, positions):
    half_rope = ROPE // 2
    frequency = theta ** (-2.0 * jnp.arange(half_rope, dtype=jnp.float32) / ROPE)
    angles = positions.astype(jnp.float32)[..., None] * frequency
    cosine = jnp.cos(angles)[..., None, :]
    sine_part = jnp.sin(angles)[..., None, :]
    front_half = queries[..., LATENT : LATENT + half_rope].astype(jnp.float32)
    back_half = queries[..., LATENT + half_rope :].astype(jnp.float32)
    turned = jnp.concatenate(
        [front_half * cosine - back_half * sine_part, back_half * cosine + front_half * sine_part],
        axis=-1,
    )
    return jnp.concatenate([queries[..., :LATENT], turned.astype(jnp.bfloat16)], axis=-1)


def score_rows(blocks, limits, cache_rows, first_place):
    scores = lax.dot_general(
        blocks, cache_rows, (((1,), (1,)), ((), ())), preferred_element_type=jnp.float32
    ) * (NOPE + ROPE) ** (-0.5)
    places = first_place + jnp.arange(cache_rows.shape[0], dtype=jnp.int32)
    visible = places[None, :] <= limits[:, None]
    return (scores, visible)


def per_device(queries, cache, lengths, offsets, w_uv, w_out):
    head_count = queries.shape[2]
    entries = queries.shape[3]
    positions = lengths[0] - DRAFT + offsets[0]
    rotated = rotate(queries[0], positions)
    cache_rows = cache[0]
    values = cache_rows[:, :LATENT]
    first_place = lax.axis_index("ctx") * cache_rows.shape[0]
    devices_ctx = lax.axis_size("ctx")
    blocks = rotated.reshape(DRAFT * head_count, entries)
    gathered = lax.all_gather(blocks, "ctx", axis=0, tiled=True)
    limits = jnp.tile(jnp.repeat(positions, head_count), devices_ctx)
    scores, visible = score_rows(gathered, limits, cache_rows, first_place)
    maxima = jnp.max(jnp.where(visible, scores, negative), axis=1)
    peaks = taken_together(maxima, "ctx")
    weights = jnp.where(visible, jnp.exp(scores - peaks[:, None]), 0.0)
    totals = jnp.sum(weights, axis=1)
    numerators = jnp.dot(weights.astype(jnp.bfloat16), values, preferred_element_type=jnp.float32)
    numerators, totals = sent_together((numerators, totals), "ctx", 0, 1)
    attended = (
        (numerators / totals[:, None]).astype(jnp.bfloat16).reshape(DRAFT, head_count, LATENT)
    )
    head_values = jnp.einsum(
        "thl,hlv->thv", attended, w_uv, preferred_element_type=jnp.float32
    ).astype(jnp.bfloat16)
    head_values = head_values.reshape(DRAFT, head_count * head_values.shape[2])
    every_token = collect(head_values, "seq", 0)
    return sent_and_summed(
        jnp.dot(every_token, w_out, preferred_element_type=jnp.float32), ("ctx", "head"), 0
    ).astype(jnp.bfloat16)


def solution(mesh):
    in_specs = (
        P(("groups", "seq"), None, ("ctx", "head"), None),
        P(("groups", "seq"), "ctx", None),
        P(("groups", "seq")),
        P(("groups", "seq"), None),
        P(("ctx", "head"), None, None),
        P(("ctx", "head"), "seq"),
    )
    out_specs = P(("groups", "ctx", "head"), "seq")
    return jax.shard_map(
        per_device, mesh=mesh, in_specs=in_specs, out_specs=out_specs, check_vma=False
    )
```

profile of v0, /device:TPU:80, one launch (start us, length us, event | category | flops | bytes accessed | tf_op | source)
XLA Modules:
  0.0 169.3 jit_solution(17803864457834293212)
XLA Ops:
  0.0 0.0 copy-start
  0.7 0.7 fusion.19
  1.4 0.1 broadcast_in_dim.15
  1.5 0.1 tile.7
  1.6 0.1 le.16
  1.7 0.7 slice.16
  2.4 0.1 multiply_cosine_fusion
  2.5 0.8 fusion.14
  3.3 0.1 pad_maximum_fusion.1
  3.4 69.8 %all_gather.3 = bf16[256,576]{1,0:T(8,128)(2,1)S(1)} all-gather(bf16[16,576]{1,0:T(8,128)(2,1)S(1)} %reshape.103), channel_id=1, replica_groups=mesh['groups'=2,'ctx'=16,'seq'=8,'head'=2] {'ctx'}, dimensions={0}, use_global_device_ids=true | all-gather | bytes 313344 | tf_op jit(solution)/shard_map/all_gather | solution.py:97
  73.3 5.2 %fusion = (f32[256]{0:T(256)S(1)}, f32[256,3072]{1,0:T(8,128)}) fusion(s32[3072]{0:T(1024)S(1)} %iota_add_fusion, s32[256]{0:T(256)S(1)} %le.16, bf16[256,576]{1,0:T(8,128)(2,1)S(1)} %all_gather.3, bf16[1,3072,576]{1,2,0:T(8,128)(2,1)} %param.7), kind=kOutput, calls=%fused_computation.3 | convolution fusion | flops 909115136 | bytes 6993920 | tf_op jit(solution)/shard_map/dot_general | solution.py:79
  78.5 15.5 %all_to_all.21 = f32[16,1,256]{2,1,0:T(1,128)S(1)} all-to-all(f32[16,1,256]{2,1,0:T(1,128)S(1)} %broadcast_in_dim.31), channel_id=1, replica_groups=mesh['groups'=2,'ctx'=16,'seq'=8,'head'=2] {'ctx'}, dimensions={0} | all-to-all | bytes 32768 | tf_op jit(solution)/shard_map/all_to_all | solution.py:20
  94.0 0.0 copy-start.1
  94.0 2.8 %fusion.3 = f32[256]{0:T(256)S(1)} fusion(f32[256,3072]{1,0:T(8,128)} %get-tuple-element.12, f32[256]{0:T(256)S(1)} %reduce_max.19, s32[3072]{0:T(1024)S(1)} %iota_add_fusion, s32[256]{0:T(256)S(1)} %le.16), kind=kLoop, calls=%fused_computation.6 | loop fusion | flops 3145472 | bytes 3161088 | tf_op jit(solution)/shard_map/reduce_sum | solution.py:103
  96.8 0.0 copy-done.1
  96.8 3.0 %fusion.1 = f32[256,512]{1,0:T(8,128)S(1)} fusion(bf16[3072,576]{0,1:T(8,128)(2,1)} %bitcast.24, f32[256,3072]{1,0:T(8,128)S(1)} %copy-done.1, f32[256]{0:T(256)S(1)} %reduce_max.19, s32[3072]{0:T(1024)S(1)} %iota_add_fusion, s32[256]{0:T(256)S(1)} %le.16), kind=kOutput, calls=%fused_computation.4 | convolution fusion | flops 808452096 | bytes 6830080 | tf_op jit(solution)/shard_map/dot_general | solution.py:104
  99.8 0.0 copy-start.2
  99.8 0.2 concatenate.18
  100.0 0.1 pad_maximum_fusion
  100.1 31.9 %all_to_all.22 = f32[16,16,513]{2,1,0:T(8,128)S(1)} all-to-all(f32[16,16,513]{2,1,0:T(8,128)S(1)} %pad_maximum_fusion), channel_id=1, replica_groups=mesh['groups'=2,'ctx'=16,'seq'=8,'head'=2] {'ctx'}, dimensions={0} | all-to-all | bytes 1050624 | tf_op jit(solution)/shard_map/all_to_all | solution.py:37
  132.1 0.1 slice_reduce_fusion
  132.2 0.1 fusion.11
  132.3 0.0 copy-done.2
  132.3 0.2 fusion.10
  132.5 15.1 %all_to_all.23 = bf16[8,4,512]{2,1,0:T(4,128)(2,1)S(1)} all-to-all(bf16[8,4,512]{2,1,0:T(4,128)(2,1)S(1)} %broadcast_in_dim.34), channel_id=1, replica_groups=mesh['groups'=2,'ctx'=16,'seq'=8,'head'=2] {'seq'}, dimensions={0} | all-to-all | bytes 65536 | tf_op jit(solution)/shard_map/all_to_all | solution.py:20
  147.6 0.0 copy-done
  147.7 0.3 convolution_bitcast_fusion
  147.9 0.1 copy.21
  148.1 20.6 %all_to_all.24 = f32[32,1,896]{2,1,0:T(1,128)S(1)} all-to-all(f32[32,1,896]{2,1,0:T(1,128)S(1)} %copy.21), channel_id=1, replica_groups=mesh['groups'=2,'ctx'=16,'seq'=8,'head'=2] {'ctx','head'}, dimensions={0} | all-to-all | bytes 229376 | tf_op jit(solution)/shard_map/all_to_all | solution.py:37
  168.7 0.1 reduce_sum.29
  168.8 0.6 convert_element_type.48
  (10 shorter events, 0.2 us)
Async XLA Ops:
  0.0 147.6 %copy-start = (bf16[512,896]{1,0:T(8,128)(2,1)S(1)}, bf16[512,896]{1,0:T(8,128)(2,1)}, u32[]{:S(2)}) copy-start(bf16[512,896]{1,0:T(8,128)(2,1)} %param.11) | copy-start | bytes 2752516
  94.0 2.8 %copy-start.1 = (f32[256,3072]{1,0:T(8,128)S(1)}, f32[256,3072]{1,0:T(8,128)}, u32[]{:S(2)}) copy-start(f32[256,3072]{1,0:T(8,128)} %get-tuple-element.12) | copy-start | bytes 9437188
  99.8 32.5 %copy-start.2 = (bf16[4,512,128]{2,1,0:T(8,128)(2,1)S(1)}, bf16[4,512,128]{2,1,0:T(8,128)(2,1)}, u32[]{:S(2)}) copy-start(bf16[4,512,128]{2,1,0:T(8,128)(2,1)} %param.10) | copy-start | bytes 1572868
where the time goes:
time: 170 us; the launch traced here: 169 us
  blocking collectives  153 us (90%)
  matrix products  8.6 us (5%)
  other arithmetic  4.82 us (3%)
  local copies, waits for them, and re-layouts  2.13 us (1%)
    all_gather x1, blocking collectives, per_device(): gathered = lax.all_gather(blocks, 'ctx', axis=0, tiled=True)  69.8 us
    all_to_all x2, blocking collectives, sent_and_summed(): lax.all_to_all(blocks, axis, split_axis=0, concat_axis=0, tiled=True)  52.5 us
    all_to_all x2, blocking collectives, copy_for_each(): lax.all_to_all(jnp.broadcast_to(value[None], (devices, *value.shape)), ax...  30.6 us
    dot_general x1, matrix products, score_rows(): lax.dot_general(blocks, cache_rows, (((1,), (1,)), ((), ())), preferred_e...  5.18 us

commit v1 on v0

--- a/solution.py
+++ b/solution.py
@@ -1,5 +1,3 @@
-import math
-
 import jax
 import jax.numpy as jnp
 from jax import lax
@@ -22,32 +20,10 @@
     )
 
 
-def taken_together(value, axis):
-    return copy_for_each(value, axis).max(axis=0)
-
-
 def cut_along(value, dim, devices):
     dims = value.shape
     blocks = value.reshape(*dims[:dim], devices, dims[dim] // devices, *dims[dim + 1 :])
     return jnp.moveaxis(blocks, dim, 0)
-
-
-def sent_and_summed(value, axis, dim):
-    blocks = cut_along(value, dim, lax.axis_size(axis))
-    arrived = lax.all_to_all(blocks, axis, split_axis=0, concat_axis=0, tiled=True)
-    return arrived.sum(axis=0)
-
-
-def sent_together(arrays, axis, dim, along):
-    widths = [math.prod(a.shape[along:]) for a in arrays]
-    both = jnp.concatenate(
-        [a.reshape(*a.shape[:along], w) for a, w in zip(arrays, widths)], axis=along
-    )
-    result = sent_and_summed(both, axis, dim)
-    blocks = jnp.split(result, [sum(widths[:k]) for k in range(1, len(widths))], axis=along)
-    return tuple(
-        (b.reshape(*result.shape[:along], *a.shape[along:]) for a, b in zip(arrays, blocks))
-    )
 
 
 def joined_along(blocks, dim):
@@ -84,6 +60,15 @@
     return (scores, visible)
 
 
+def in_pieces(value, count):
+    pieces = []
+    for _ in range(count):
+        piece = lax.reduce_precision(value, 8, 7)
+        pieces.append(piece.astype(jnp.bfloat16))
+        value = value - piece
+    return jnp.stack(pieces, axis=-1)
+
+
 def per_device(queries, cache, lengths, offsets, w_uv, w_out):
     head_count = queries.shape[2]
     entries = queries.shape[3]
@@ -93,27 +78,36 @@
     values = cache_rows[:, :LATENT]
     first_place = lax.axis_index("ctx") * cache_rows.shape[0]
     devices_ctx = lax.axis_size("ctx")
-    blocks = rotated.reshape(DRAFT * head_count, entries)
-    gathered = lax.all_gather(blocks, "ctx", axis=0, tiled=True)
+    rows = DRAFT * head_count
+    blocks = rotated.reshape(rows, entries)
+    gathered = copy_for_each(blocks, "ctx").reshape(devices_ctx * rows, entries)
     limits = jnp.tile(jnp.repeat(positions, head_count), devices_ctx)
     scores, visible = score_rows(gathered, limits, cache_rows, first_place)
     maxima = jnp.max(jnp.where(visible, scores, negative), axis=1)
-    peaks = taken_together(maxima, "ctx")
-    weights = jnp.where(visible, jnp.exp(scores - peaks[:, None]), 0.0)
+    weights = jnp.where(visible, jnp.exp(scores - maxima[:, None]), 0.0)
     totals = jnp.sum(weights, axis=1)
     numerators = jnp.dot(weights.astype(jnp.bfloat16), values, preferred_element_type=jnp.float32)
-    numerators, totals = sent_together((numerators, totals), "ctx", 0, 1)
-    attended = (
-        (numerators / totals[:, None]).astype(jnp.bfloat16).reshape(DRAFT, head_count, LATENT)
-    )
+    shares = numerators / jnp.maximum(totals, 1.0)[:, None]
+    stats = jnp.concatenate([in_pieces(maxima, 3), in_pieces(totals, 3)], axis=-1)
+    sent = jnp.concatenate([shares.astype(jnp.bfloat16), stats], axis=-1)
+    sent = sent.reshape(devices_ctx, rows, LATENT + 6)
+    arrived = lax.all_to_all(sent, "ctx", split_axis=0, concat_axis=0, tiled=True)
+    arrived = arrived.astype(jnp.float32)
+    peaks = arrived[..., LATENT : LATENT + 3].sum(axis=-1)
+    parts = arrived[..., LATENT + 3 :].sum(axis=-1)
+    parts = parts * jnp.exp(peaks - peaks.max(axis=0))
+    parts = parts / parts.sum(axis=0)
+    attended = (arrived[..., :LATENT] * parts[..., None]).sum(axis=0)
+    attended = attended.astype(jnp.bfloat16).reshape(DRAFT, head_count, LATENT)
     head_values = jnp.einsum(
         "thl,hlv->thv", attended, w_uv, preferred_element_type=jnp.float32
     ).astype(jnp.bfloat16)
     head_values = head_values.reshape(DRAFT, head_count * head_values.shape[2])
     every_token = collect(head_values, "seq", 0)
-    return sent_and_summed(
-        jnp.dot(every_token, w_out, preferred_element_type=jnp.float32), ("ctx", "head"), 0
-    ).astype(jnp.bfloat16)
+    mixed = jnp.dot(every_token, w_out, preferred_element_type=jnp.float32).astype(jnp.bfloat16)
+    mixed = cut_along(mixed, 0, lax.axis_size(("ctx", "head")))
+    mixed = lax.all_to_all(mixed, ("ctx", "head"), split_axis=0, concat_axis=0, tiled=True)
+    return mixed.astype(jnp.float32).sum(axis=0).astype(jnp.bfloat16)
 
 
 def solution(mesh):

time: 170 us -> 146 us (0.86)
  blocking collectives: 153 us -> 62.3 us
  starting transfers between devices: 0 us -> 43.7 us
  waiting for transfers between devices: 0 us -> 20.5 us
  local copies, waits for them, and re-layouts: 2.13 us -> 6.33 us
    all_gather x1 -> x0, blocking collectives: 69.8 us -> none  [per_device(): gathered = lax.all_gather(blocks, 'ctx', axis=0, tiled=True)]
    all_to_all x0 -> x1, starting transfers between devices: none -> 43.7 us  [copy_for_each(): lax.all_to_all(jnp.broadcast_to(value[None], (devices, *value.shape)), ax...]
    all_to_all x0 -> x1, waiting for transfers between devices: none -> 20.5 us  [copy_for_each(): lax.all_to_all(jnp.broadcast_to(value[None], (devices, *value.shape)), ax...]
    all_to_all x2 -> x1, blocking collectives: 30.6 us -> 15.2 us  [copy_for_each(): lax.all_to_all(jnp.broadcast_to(value[None], (devices, *value.shape)), ax...]
    all_to_all x2, blocking collectives: 52.5 us -> 47.1 us  [the longest x1 26.4 us: per_device(): lax.all_to_all(sent, 'ctx', split_axis=0, concat_axis=0, tiled=True)]
    reduce_sum x1, other arithmetic: 2.81 us -> 0.78 us  [per_device(): totals = jnp.sum(weights, axis=1)]
    unnamed x6 -> x8, local copies, waits for them, and re-layouts: 0.04 us -> 1.94 us
  transfers between devices with their start and end apart: 0 -> 1, of which waited for: 0 -> 1; matrix products, arithmetic and copies ran while one was open for 0% -> 0% of each run, Pallas kernels for 0% -> 0%
where the time goes in v1:
time: 146 us; the launch traced here: 145 us
  blocking collectives  62.3 us (43%)
  starting transfers between devices  43.7 us (30%)
  waiting for transfers between devices  20.5 us (14%)
  matrix products  7.98 us (5%)
  local copies, waits for them, and re-layouts  6.33 us (4%)
  other arithmetic  3.69 us (3%)
    all_to_all x1, starting transfers between devices, copy_for_each(): lax.all_to_all(jnp.broadcast_to(value[None], (devices, *value.shape)), ax...  43.7 us
    all_to_all x1, blocking collectives, per_device(): lax.all_to_all(sent, 'ctx', split_axis=0, concat_axis=0, tiled=True)  26.4 us
    all_to_all x1, blocking collectives, per_device(): lax.all_to_all(mixed, ('ctx', 'head'), split_axis=0, concat_axis=0, tiled...  20.7 us
    all_to_all x1, waiting for transfers between devices, copy_for_each(): lax.all_to_all(jnp.broadcast_to(value[None], (devices, *value.shape)), ax...  20.5 us
    all_to_all x1, blocking collectives, copy_for_each(): lax.all_to_all(jnp.broadcast_to(value[None], (devices, *value.shape)), ax...  15.2 us
    dot_general x1, matrix products, per_device(): jnp.dot(weights.astype(jnp.bfloat16), values, preferred_element_type=jnp....  3.9 us
    dot_general x1, matrix products, score_rows(): lax.dot_general(blocks, cache_rows, (((1,), (1,)), ((), ())), preferred_e...  3.65 us
  transfers between devices with their start and end apart: 1, of which 1 were waited for; matrix products, arithmetic and copies ran while one was open for 0% of the time, Pallas kernels for 0%

profile of v1, /device:TPU:80, one launch (start us, length us, event | category | flops | bytes accessed | tf_op | source)
XLA Modules:
  0.0 145.4 jit_solution(12485320992730535226)
XLA Ops:
  0.0 0.0 copy-start
  0.7 0.7 slice.28
  1.5 0.7 fusion.35
  2.1 0.1 multiply_cosine_fusion
  2.2 0.8 fusion.25
  3.1 0.1 pad_maximum_fusion
  3.2 0.7 broadcast_in_dim.36
  3.9 43.7 %all-to-all-start = ((bf16[16,16,576]{2,1,0:T(8,128)(2,1)}), bf16[16,16,576]{2,1,0:T(8,128)(2,1)S(1)}, u32[]{:S(2)}, u32[]{:S(2)}) async-start(bf16[16,16,576]{2,1,0:T(8,128)(2,1)} %broadcast_in_dim.36), calls=%async_computation | async-start | bytes 655360 | tf_op jit(solution)/shard_map/all_to_all | solution.py:18
  47.6 0.1 broadcast_in_dim.17
  47.7 0.1 tile.7
  47.8 0.1 le.16
  47.9 20.5 %all-to-all-done = bf16[16,16,576]{2,1,0:T(8,128)(2,1)S(1)} async-done(((bf16[16,16,576]{2,1,0:T(8,128)(2,1)}), bf16[16,16,576]{2,1,0:T(8,128)(2,1)S(1)}, u32[]{:S(2)}, u32[]{:S(2)}) %all-to-all-start) | async-done | bytes 294944 | tf_op jit(solution)/shard_map/all_to_all | solution.py:18
  68.4 3.6 %fusion = (f32[256]{0:T(256)S(1)}, f32[256,3072]{1,0:T(8,128)S(1)}) fusion(s32[3072]{0:T(1024)S(1)} %iota_add_fusion, s32[256]{0:T(256)S(1)} %le.16, bf16[256,576]{1,0:T(8,128)(2,1)S(1)} %bitcast.22, bf16[1,3072,576]{1,2,0:T(8,128)(2,1)} %param.7), kind=kOutput, calls=%fused_computation.3 | convolution fusion | flops 909115136 | bytes 6993920 | tf_op jit(solution)/shard_map/dot_general | solution.py:55
  72.1 0.0 copy-start.1
  72.1 1.7 %copy-done.1 = f32[256,3072]{1,0:T(8,128)} copy-done((f32[256,3072]{1,0:T(8,128)}, f32[256,3072]{1,0:T(8,128)S(1)}, u32[]{:S(2)}) %copy-start.1) | copy-done | bytes 3145752
  73.7 0.8 fusion.3
  74.5 0.1 reduce_sum.62
  74.6 0.1 reduce_max.21
  74.7 0.2 copy.17
  74.9 0.2 copy.18
  75.1 0.2 copy.19
  75.3 0.2 copy.14
  75.5 0.2 copy.15
  75.6 0.2 copy.16
  75.8 3.9 %fusion.17 = bf16[256,512]{1,0:T(8,128)(2,1)S(1)} fusion(bf16[3072,576]{0,1:T(8,128)(2,1)} %bitcast.26, f32[256,3072]{1,0:T(8,128)} %copy-done.1, f32[256]{0:T(256)S(1)} %get-tuple-element.19, s32[3072]{0:T(1024)S(1)} %iota_add_fusion, s32[256]{0:T(256)S(1)} %le.16, f32[256]{0:T(256)S(1)} %broadcast_maximum_fusion), kind=kOutput, calls=%fused_computation.17 | convolution fusion | flops 808714240 | bytes 6568960 | tf_op jit(solution)/shard_map/dot_general | solution.py:89
  79.7 0.0 copy-start.2
  79.7 0.2 concatenate.14
  80.0 26.4 %all_to_all.20 = bf16[16,16,518]{2,1,0:T(8,128)(2,1)S(1)} all-to-all(bf16[16,16,518]{2,1,0:T(8,128)(2,1)S(1)} %concatenate.14), channel_id=1, replica_groups=mesh['groups'=2,'ctx'=16,'seq'=8,'head'=2] {'ctx'}, dimensions={0} | all-to-all | bytes 530432 | tf_op jit(solution)/shard_map/all_to_all | solution.py:94
  106.4 0.2 slice_reduce_fusion
  106.7 0.1 fusion.22
  106.8 0.0 copy-done.2
  106.8 0.2 fusion.11
  107.0 15.2 %all_to_all.21 = bf16[8,4,512]{2,1,0:T(4,128)(2,1)S(1)} all-to-all(bf16[8,4,512]{2,1,0:T(4,128)(2,1)S(1)} %broadcast_in_dim.40), channel_id=1, replica_groups=mesh['groups'=2,'ctx'=16,'seq'=8,'head'=2] {'seq'}, dimensions={0} | all-to-all | bytes 65536 | tf_op jit(solution)/shard_map/all_to_all | solution.py:18
  122.2 0.0 copy-done
  122.2 0.3 fusion.10
  122.5 0.5 broadcast.70
  123.0 0.7 reduce.2
  123.7 0.1 reshape.230
  123.8 20.7 %all_to_all.22 = bf16[32,2,448]{2,1,0:T(2,128)(2,1)S(1)} all-to-all(bf16[32,2,448]{2,1,0:T(2,128)(2,1)S(1)} %reshape.230), channel_id=1, replica_groups=mesh['groups'=2,'ctx'=16,'seq'=8,'head'=2] {'ctx','head'}, dimensions={0} | all-to-all | bytes 114688 | tf_op jit(solution)/shard_map/all_to_all | solution.py:109
  144.5 0.1 reshape.231
  144.6 0.1 reduce_sum.67
  144.8 0.6 reduce_sum.68
  (14 shorter events, 0.2 us)
Async XLA Ops:
  0.0 122.2 %copy-start = (bf16[512,896]{1,0:T(8,128)(2,1)S(1)}, bf16[512,896]{1,0:T(8,128)(2,1)}, u32[]{:S(2)}) copy-start(bf16[512,896]{1,0:T(8,128)(2,1)} %param.11) | copy-start | bytes 2752516
  3.9 64.5 %all-to-all-start = ((bf16[16,16,576]{2,1,0:T(8,128)(2,1)}), bf16[16,16,576]{2,1,0:T(8,128)(2,1)S(1)}, u32[]{:S(2)}, u32[]{:S(2)}) async-start(bf16[16,16,576]{2,1,0:T(8,128)(2,1)} %broadcast_in_dim.36), calls=%async_computation | async-start | bytes 655360 | tf_op jit(solution)/shard_map/all_to_all | solution.py:18
  72.1 1.7 %copy-start.1 = (f32[256,3072]{1,0:T(8,128)}, f32[256,3072]{1,0:T(8,128)S(1)}, u32[]{:S(2)}) copy-start(f32[256,3072]{1,0:T(8,128)S(1)} %get-tuple-element.20) | copy-start | bytes 9437188
  79.7 27.1 %copy-start.2 = (bf16[4,512,128]{2,1,0:T(8,128)(2,1)S(1)}, bf16[4,512,128]{2,1,0:T(8,128)(2,1)}, u32[]{:S(2)}) copy-start(bf16[4,512,128]{2,1,0:T(8,128)(2,1)} %param.10) | copy-start | bytes 1572868

commit v2 on v0

v2 whole, which is shorter than its diff:
```python
import functools
import math

import jax
import jax.numpy as jnp
import numpy as np
from jax import lax
from jax.experimental import pallas as pl
from jax.experimental.pallas import tpu as pltpu
from jax.sharding import PartitionSpec as P

LATENT = 512
ROPE = 64
NOPE = 128
DRAFT = 4
LANES = 128
TILE = 256

theta = 10000.0
negative = -1e30
scale = (NOPE + ROPE) ** (-0.5)
scale_log2 = scale * math.log2(math.e)

F32 = jnp.float32
BF16 = jnp.bfloat16
VMEM = pl.BlockSpec(memory_space=pltpu.VMEM)
SMEM = pl.BlockSpec(memory_space=pltpu.SMEM)
LATENT_BLOCKS = LATENT // LANES


def packed_angles(positions, rows):
    half = ROPE // 2
    frequency = np.float32(theta ** (-2.0 * np.arange(half) / ROPE))
    by_row = jnp.repeat(positions.astype(F32), rows // DRAFT).reshape(2, rows // 2)
    angles = by_row[:, :, None] * jnp.asarray(np.tile(frequency, 2))
    return jnp.concatenate([angles[0], angles[1]], axis=-1)


def rotation_tables(positions, rows):
    angles = packed_angles(positions, rows)
    lane = lax.broadcasted_iota(jnp.int32, angles.shape, 1)
    sign = jnp.where(lane % ROPE < ROPE // 2, -1.0, 1.0).astype(F32)
    return jnp.stack([jnp.cos(angles), jnp.sin(angles) * sign])


def pack_kernel(queries_ref, sent_ref):
    rows = jnp.concatenate([queries_ref[0, t].astype(F32) for t in range(DRAFT)], axis=0)
    half = rows.shape[0] // 2
    parts = [rows[:, j * LANES : (j + 1) * LANES] for j in range(LATENT_BLOCKS)]
    rope = rows[:, LATENT : LATENT + ROPE]
    parts.append(jnp.concatenate([rope[:half], rope[half:]], axis=1))
    message = jnp.concatenate(parts, axis=0).astype(BF16)
    for d in range(sent_ref.shape[0]):
        sent_ref[d] = message


def pieces_of(value):
    first = value.astype(BF16).astype(F32)
    second = (value - first).astype(BF16).astype(F32)
    third = (value - first - second).astype(BF16).astype(F32)
    return first, second, third


def attend_kernel(scalars_ref, tables_ref, arrived_ref, cache_ref, sent_ref, q_ref, s_ref, p_ref):
    devices = arrived_ref.shape[0]
    places = cache_ref.shape[0]
    rows = q_ref.shape[0] // devices
    half = rows // 2
    for j in range(LATENT_BLOCKS):
        block = arrived_ref[:, j * rows : (j + 1) * rows, :]
        q_ref[:, j * LANES : (j + 1) * LANES] = block.reshape(devices * rows, LANES)
    x = arrived_ref[:, LATENT_BLOCKS * rows :, :].astype(F32).reshape(devices * half, LANES)
    lane = lax.broadcasted_iota(jnp.int32, x.shape, 1)
    partner = jnp.where(
        lane % ROPE < ROPE // 2,
        pltpu.roll(x, LANES - ROPE // 2, 1),
        pltpu.roll(x, ROPE // 2, 1),
    )
    shape3 = (devices, half, LANES)
    turned = x.reshape(shape3) * tables_ref[0][None] + partner.reshape(shape3) * tables_ref[1][None]
    swapped = pltpu.roll(turned.reshape(devices * half, LANES), ROPE, 1).reshape(shape3)
    rope = jnp.stack([turned, swapped], axis=1).reshape(devices * rows, LANES)
    q_ref[:, LATENT:] = rope[:, :ROPE].astype(BF16)

    row = lax.broadcasted_iota(jnp.int32, (devices * rows, TILE), 0) % rows
    limits = jnp.full(row.shape, scalars_ref[0], jnp.int32)
    for t in range(1, DRAFT):
        limits = jnp.where(row >= t * (rows // DRAFT), scalars_ref[t], limits)
    limits = limits - lax.broadcasted_iota(jnp.int32, row.shape, 1)
    top = jnp.full((devices * rows, LANES), negative, F32)
    for i in range(places // TILE):
        scores = lax.dot_general(
            q_ref[...],
            cache_ref[i * TILE : (i + 1) * TILE, :],
            (((1,), (1,)), ((), ())),
            preferred_element_type=F32,
        )
        scores = jnp.where(limits >= i * TILE, scores, negative)
        s_ref[:, i * TILE : (i + 1) * TILE] = scores
        for j in range(TILE // LANES):
            top = jnp.maximum(top, scores[:, j * LANES : (j + 1) * LANES])
    peak = jnp.max(top, axis=1, keepdims=True)
    total = jnp.zeros((devices * rows, LANES), F32)
    for i in range(places // TILE):
        weights = jnp.exp2((s_ref[:, i * TILE : (i + 1) * TILE] - peak) * scale_log2)
        for j in range(TILE // LANES):
            total += weights[:, j * LANES : (j + 1) * LANES]
        p_ref[:, i * TILE : (i + 1) * TILE] = weights.astype(BF16)
    total = jnp.sum(total, axis=1, keepdims=True)
    share = jnp.dot(p_ref[...], cache_ref[:, :LATENT], preferred_element_type=F32) / total
    for j in range(LATENT_BLOCKS):
        block = share[:, j * LANES : (j + 1) * LANES].astype(BF16)
        sent_ref[:, j * rows : (j + 1) * rows, :] = block.reshape(devices, rows, LANES)
    lane = lax.broadcasted_iota(jnp.int32, (devices * rows, LANES), 1)
    stats = jnp.zeros(lane.shape, F32)
    for k, piece in enumerate((*pieces_of(peak), *pieces_of(total))):
        stats = jnp.where(lane % ROPE == k, piece, stats)
    stats = stats.reshape(devices, 2, half, LANES)
    lane = lax.broadcasted_iota(jnp.int32, (devices, half, LANES), 2)
    sent_ref[:, LATENT_BLOCKS * rows :, :] = jnp.where(
        lane < ROPE, stats[:, 0], stats[:, 1]
    ).astype(BF16)


def combine_kernel(arrived_ref, w_uv_ref, sent_ref):
    devices, _, _ = arrived_ref.shape
    heads = w_uv_ref.shape[0]
    rows = DRAFT * heads
    half = rows // 2
    packed = arrived_ref[:, LATENT_BLOCKS * rows :, :].astype(F32)
    stats = jnp.concatenate(
        [packed, pltpu.roll(packed.reshape(devices * half, LANES), ROPE, 1).reshape(packed.shape)],
        axis=1,
    )
    peaks = stats[:, :, 0:1] + stats[:, :, 1:2] + stats[:, :, 2:3]
    parts = stats[:, :, 3:4] + stats[:, :, 4:5] + stats[:, :, 5:6]
    parts = parts * jnp.exp2((peaks - jnp.max(peaks, axis=0, keepdims=True)) * scale_log2)
    parts = parts / jnp.sum(parts, axis=0, keepdims=True)
    blocks = []
    for j in range(LATENT_BLOCKS):
        block = arrived_ref[:, j * rows : (j + 1) * rows, :].astype(F32)
        blocks.append(jnp.sum(block * parts, axis=0))
    attended = jnp.concatenate(blocks, axis=1).astype(BF16)
    row = lax.broadcasted_iota(jnp.int32, (rows, w_uv_ref.shape[2]), 0)
    values = []
    for h in range(heads):
        value = jnp.dot(attended, w_uv_ref[h], preferred_element_type=F32)
        values.append(jnp.where(row % heads == h, value, 0.0))
    values = jnp.concatenate(values, axis=1).astype(BF16)
    token = lax.broadcasted_iota(jnp.int32, (DRAFT, rows), 0)
    member = lax.broadcasted_iota(jnp.int32, (DRAFT, rows), 1) // heads
    pick = (token == member).astype(BF16)
    values = jnp.dot(pick, values, preferred_element_type=F32).astype(BF16)
    for d in range(sent_ref.shape[0]):
        sent_ref[d] = values


def per_device(queries, cache, lengths, offsets, w_uv, w_out):
    heads = queries.shape[2]
    rows = DRAFT * heads
    places = cache.shape[1]
    devices_ctx = lax.axis_size("ctx")
    devices_seq = lax.axis_size("seq")
    message = LATENT_BLOCKS * rows + rows // 2
    positions = lengths[0] - DRAFT + offsets[0]
    sent = pl.pallas_call(
        pack_kernel,
        out_shape=jax.ShapeDtypeStruct((devices_ctx, message, LANES), BF16),
        in_specs=[VMEM],
        out_specs=VMEM,
        name="pack",
    )(queries)
    arrived = lax.all_to_all(sent, "ctx", 0, 0, tiled=True)
    scalars = positions - lax.axis_index("ctx") * places
    all_rows = devices_ctx * rows
    sent = pl.pallas_call(
        attend_kernel,
        out_shape=jax.ShapeDtypeStruct((devices_ctx, message, LANES), BF16),
        in_specs=[SMEM, VMEM, VMEM, VMEM],
        out_specs=VMEM,
        scratch_shapes=[
            pltpu.VMEM((all_rows, LATENT + ROPE), BF16),
            pltpu.VMEM((all_rows, places), F32),
            pltpu.VMEM((all_rows, places), BF16),
        ],
        compiler_params=pltpu.CompilerParams(vmem_limit_bytes=24 * 1024 * 1024),
        name="attend",
    )(scalars, rotation_tables(positions, rows), arrived, cache[0])
    arrived = lax.all_to_all(sent, "ctx", 0, 0, tiled=True)
    sent = pl.pallas_call(
        combine_kernel,
        out_shape=jax.ShapeDtypeStruct((devices_seq, DRAFT, heads * w_uv.shape[2]), BF16),
        in_specs=[VMEM, VMEM],
        out_specs=VMEM,
        name="combine",
    )(arrived, w_uv)
    every_token = lax.all_to_all(sent, "seq", 0, 0, tiled=True)
    every_token = every_token.reshape(devices_seq * DRAFT, w_out.shape[0])
    mixed = jnp.dot(every_token, w_out, preferred_element_type=F32).astype(BF16)
    mixed = lax.all_to_all(mixed[:, None, :], ("ctx", "head"), 0, 0, tiled=True)
    return mixed.astype(F32).sum(axis=0).astype(BF16)


def solution(mesh):
    in_specs = (
        P(("groups", "seq"), None, ("ctx", "head"), None),
        P(("groups", "seq"), "ctx", None),
        P(("groups", "seq")),
        P(("groups", "seq"), None),
        P(("ctx", "head"), None, None),
        P(("ctx", "head"), "seq"),
    )
    out_specs = P(("groups", "ctx", "head"), "seq")
    return jax.shard_map(
        per_device, mesh=mesh, in_specs=in_specs, out_specs=out_specs, check_vma=False
    )
```

time: 170 us -> 137 us (0.81)
  blocking collectives: 153 us -> 61.3 us
  starting transfers between devices: 0 us -> 43.8 us
  waiting for transfers between devices: 0 us -> 11.4 us
  matrix products: 8.6 us -> 0.26 us
  local copies, waits for them, and re-layouts: 2.13 us -> 9.85 us
  Pallas kernels: 0 us -> 7.5 us
  other arithmetic: 4.82 us -> 1.66 us
    all_gather x1 -> x0, blocking collectives: 69.8 us -> none  [per_device(): gathered = lax.all_gather(blocks, 'ctx', axis=0, tiled=True)]
    all_to_all x0 -> x1, starting transfers between devices: none -> 43.8 us  [per_device(): arrived = lax.all_to_all(sent, 'ctx', 0, 0, tiled=True)]
    all_to_all x4 -> x3, blocking collectives: 83.2 us -> 61.3 us  [the longest x1 25.4 us: per_device(): arrived = lax.all_to_all(sent, 'ctx', 0, 0, tiled=True)]
    all_to_all x0 -> x1, waiting for transfers between devices: none -> 11.4 us  [per_device(): arrived = lax.all_to_all(sent, 'ctx', 0, 0, tiled=True)]
    unnamed x6 -> x11, local copies, waits for them, and re-layouts: 0.04 us -> 8.48 us
    dot_general x4 -> x1, matrix products: 8.6 us -> 0.26 us  [per_device(): mixed = jnp.dot(every_token, w_out, preferred_element_type=F32).astype(BF16)]
    pallas_call x0 -> x3, Pallas kernels: none -> 7.5 us  [the longest x1 3.45 us: per_device(): pl.pallas_call(attend_kernel, out_shape=jax.ShapeDtypeStruct((devices_ctx...]
    reduce_sum x3 -> x1, other arithmetic: 2.95 us -> 0.12 us  [per_device(): return mixed.astype(F32).sum(axis=0).astype(BF16)]
  transfers between devices with their start and end apart: 0 -> 1, of which waited for: 0 -> 1; matrix products, arithmetic and copies ran while one was open for 0% -> 5% of each run, Pallas kernels for 0% -> 0%
where the time goes in v2:
time: 137 us
  blocking collectives  61.3 us (45%)
  starting transfers between devices  43.8 us (32%)
  waiting for transfers between devices  11.4 us (8%)
  local copies, waits for them, and re-layouts  9.85 us (7%)
  Pallas kernels  7.5 us (5%)
  other arithmetic  1.66 us (1%)
    all_to_all x1, starting transfers between devices, per_device(): arrived = lax.all_to_all(sent, 'ctx', 0, 0, tiled=True)  43.8 us
    all_to_all x1, blocking collectives, per_device(): arrived = lax.all_to_all(sent, 'ctx', 0, 0, tiled=True)  25.4 us
    all_to_all x1, blocking collectives, per_device(): mixed = lax.all_to_all(mixed[:, None, :], ('ctx', 'head'), 0, 0, tiled=True)  20.5 us
    all_to_all x1, blocking collectives, per_device(): every_token = lax.all_to_all(sent, 'seq', 0, 0, tiled=True)  15.3 us
    all_to_all x1, waiting for transfers between devices, per_device(): arrived = lax.all_to_all(sent, 'ctx', 0, 0, tiled=True)  11.4 us
    unnamed x11, local copies, waits for them, and re-layouts  8.48 us
    pallas_call x1, Pallas kernels, per_device(): pl.pallas_call(attend_kernel, out_shape=jax.ShapeDtypeStruct((devices_ctx...  3.45 us
  transfers between devices with their start and end apart: 1, of which 1 were waited for; matrix products, arithmetic and copies ran while one was open for 5% of the time, Pallas kernels for 0%

profile of v2, /device:TPU:80, one launch (start us, length us, event | category | flops | bytes accessed | tf_op | source)
XLA Modules:
  0.0 136.5 jit_solution(11818340421564973849)
XLA Ops:
  0.0 0.0 copy-start
  0.0 1.6 %pack.1 = bf16[16,72,128]{2,1,0:T(8,128)(2,1)} custom-call(bf16[1,4,4,576]{3,2,1,0:T(4,128)(2,1)} %queries_ref.1), custom_call_target="tpu_custom_call" | custom-call | tf_op jit(solution)/shard_map/pack/pallas_call | solution.py:166
  1.6 0.0 copy-start.2
  1.6 43.8 %all-to-all-start = ((bf16[16,72,128]{2,1,0:T(8,128)(2,1)}), bf16[16,72,128]{2,1,0:T(8,128)(2,1)S(1)}, u32[]{:S(2)}, u32[]{:S(2)}) async-start(bf16[16,72,128]{2,1,0:T(8,128)(2,1)} %pack.1), calls=%async_computation | async-start | bytes 589824 | tf_op jit(solution)/shard_map/all_to_all | solution.py:173
  45.4 0.0 copy-start.3
  46.1 0.7 convert_reduce_fusion
  46.8 0.1 convert_element_type.13
  46.9 0.1 broadcast_in_dim.17
  46.9 0.1 broadcast_in_dim.18
  47.0 6.1 %copy.9 = bf16[1,3072,576]{2,1,0:T(8,128)(2,1)} copy(bf16[1,3072,576]{1,2,0:T(8,128)(2,1)} %param.8) | data formatting | bytes 7077888 | tf_op args[1]
  53.1 0.0 copy-done.2
  53.1 0.1 broadcast_multiply_fusion
  53.2 0.1 fusion.1
  53.3 0.0 copy-done.3
  53.4 11.4 %all-to-all-done.arrived_ref = bf16[16,72,128]{2,1,0:T(8,128)(2,1)S(1)} async-done(((bf16[16,72,128]{2,1,0:T(8,128)(2,1)}), bf16[16,72,128]{2,1,0:T(8,128)(2,1)S(1)}, u32[]{:S(2)}, u32[]{:S(2)}) %all-to-all-start) | async-done | bytes 294944 | tf_op jit(solution)/shard_map/all_to_all | solution.py:173
  64.7 0.0 copy-start.1
  64.7 2.1 %copy-done.1 = bf16[1,3072,576]{2,1,0:T(8,128)(2,1)S(1)} copy-done((bf16[1,3072,576]{2,1,0:T(8,128)(2,1)S(1)}, bf16[1,3072,576]{2,1,0:T(8,128)(2,1)}, u32[]{:S(2)}) %copy-start.1) | copy-done | bytes 3538968
  66.9 3.4 %attend.1 = bf16[16,72,128]{2,1,0:T(8,128)(2,1)S(1)} custom-call(s32[4]{0:T(128)S(1)} %subtract_bitcast_fusion.scalars_ref, f32[2,8,128]{2,1,0:T(8,128)S(1)} %pad_maximum_fusion.tables_ref, bf16[16,72,128]{2,1,0:T(8,128)(2,1)S(1)} %all-to-all-done.arrived_ref, bf16[3072,576]{1,0:T(8,128)(2,1)S(1)} %bitcast.8), custom_call_target="tpu_custom_call" | custom-call | tf_op jit(solution)/shard_map/attend/pallas_call | solution.py:176
  70.3 25.4 %all_to_all.20.arrived_ref = bf16[16,72,128]{2,1,0:T(8,128)(2,1)} all-to-all(bf16[16,72,128]{2,1,0:T(8,128)(2,1)S(1)} %attend.1), channel_id=1, replica_groups=mesh['groups'=2,'ctx'=16,'seq'=8,'head'=2] {'ctx'}, dimensions={0} | all-to-all | bytes 589824 | tf_op jit(solution)/shard_map/all_to_all | solution.py:189
  95.8 2.5 %combine.1 = bf16[8,4,512]{2,1,0:T(4,128)(2,1)} custom-call(bf16[16,72,128]{2,1,0:T(8,128)(2,1)} %all_to_all.20.arrived_ref, bf16[4,512,128]{2,1,0:T(8,128)(2,1)} %w_uv_ref.1), custom_call_target="tpu_custom_call" | custom-call | tf_op jit(solution)/shard_map/combine/pallas_call | solution.py:190
  98.2 15.3 %all_to_all.21 = bf16[8,4,512]{2,1,0:T(4,128)(2,1)S(1)} all-to-all(bf16[8,4,512]{2,1,0:T(4,128)(2,1)} %combine.1), channel_id=1, replica_groups=mesh['groups'=2,'ctx'=16,'seq'=8,'head'=2] {'seq'}, dimensions={0} | all-to-all | bytes 65536 | tf_op jit(solution)/shard_map/all_to_all | solution.py:197
  113.6 0.0 copy-done
  113.6 0.3 fusion
  113.8 0.5 broadcast.123
  114.4 0.7 reduce.6
  115.0 0.1 reshape.154
  115.1 20.5 %all_to_all.22 = bf16[32,2,448]{2,1,0:T(2,128)(2,1)S(1)} all-to-all(bf16[32,2,448]{2,1,0:T(2,128)(2,1)S(1)} %reshape.154), channel_id=1, replica_groups=mesh['groups'=2,'ctx'=16,'seq'=8,'head'=2] {'ctx','head'}, dimensions={0} | all-to-all | bytes 114688 | tf_op jit(solution)/shard_map/all_to_all | solution.py:200
  135.7 0.1 reshape.155
  135.8 0.1 reduce_sum.14
  135.9 0.6 reduce_sum.15
  (6 shorter events, 0.0 us)
Async XLA Ops:
  0.0 113.6 %copy-start = (bf16[512,896]{1,0:T(8,128)(2,1)S(1)}, bf16[512,896]{1,0:T(8,128)(2,1)}, u32[]{:S(2)}) copy-start(bf16[512,896]{1,0:T(8,128)(2,1)} %param.12) | copy-start | bytes 2752516
  1.6 51.5 %copy-start.2 = (f32[64]{0:T(128)S(1)}, f32[64]{0:T(128)}, u32[]{:S(2)}) copy-start(f32[64]{0:T(128)} %constant.38.clone) | copy-start | bytes 772
  1.6 63.1 %all-to-all-start = ((bf16[16,72,128]{2,1,0:T(8,128)(2,1)}), bf16[16,72,128]{2,1,0:T(8,128)(2,1)S(1)}, u32[]{:S(2)}, u32[]{:S(2)}) async-start(bf16[16,72,128]{2,1,0:T(8,128)(2,1)} %pack.1), calls=%async_computation | async-start | bytes 589824 | tf_op jit(solution)/shard_map/all_to_all | solution.py:173
  45.4 7.9 %copy-start.3 = (s32[1,4]{1,0:T(1,128)S(1)}, s32[1,4]{1,0:T(1,128)}, u32[]{:S(2)}) copy-start(s32[1,4]{1,0:T(1,128)} %param.10) | copy-start | bytes 52
  64.7 2.1 %copy-start.1 = (bf16[1,3072,576]{2,1,0:T(8,128)(2,1)S(1)}, bf16[1,3072,576]{2,1,0:T(8,128)(2,1)}, u32[]{:S(2)}) copy-start(bf16[1,3072,576]{2,1,0:T(8,128)(2,1)} %copy.9) | copy-start | bytes 10616836

commit v3 on v2

--- a/solution.py
+++ b/solution.py
@@ -15,6 +15,7 @@
 DRAFT = 4
 LANES = 128
 TILE = 256
+COVER = 1 << 24
 
 theta = 10000.0
 negative = -1e30
@@ -38,9 +39,15 @@
 
 def rotation_tables(positions, rows):
     angles = packed_angles(positions, rows)
-    lane = lax.broadcasted_iota(jnp.int32, angles.shape, 1)
-    sign = jnp.where(lane % ROPE < ROPE // 2, -1.0, 1.0).astype(F32)
-    return jnp.stack([jnp.cos(angles), jnp.sin(angles) * sign])
+    return pl.pallas_call(
+        tables_kernel,
+        out_shape=jax.ShapeDtypeStruct((2, *angles.shape), F32),
+        in_specs=[VMEM, VMEM],
+        out_specs=VMEM,
+        compiler_params=limited(4),
+        cost_estimate=pl.CostEstimate(flops=COVER * 1000, bytes_accessed=COVER, transcendentals=0),
+        name="tables",
+    )(jnp.cos(angles), jnp.sin(angles))
 
 
 def pack_kernel(queries_ref, sent_ref):
@@ -54,6 +61,12 @@
         sent_ref[d] = message
 
 
+def tables_kernel(cosine_ref, sine_ref, tables_ref):
+    lane = lax.broadcasted_iota(jnp.int32, cosine_ref.shape, 1)
+    tables_ref[0] = cosine_ref[...]
+    tables_ref[1] = jnp.where(lane % ROPE < ROPE // 2, -sine_ref[...], sine_ref[...])
+
+
 def pieces_of(value):
     first = value.astype(BF16).astype(F32)
     second = (value - first).astype(BF16).astype(F32)
@@ -63,7 +76,7 @@
 
 def attend_kernel(scalars_ref, tables_ref, arrived_ref, cache_ref, sent_ref, q_ref, s_ref, p_ref):
     devices = arrived_ref.shape[0]
-    places = cache_ref.shape[0]
+    places = cache_ref.shape[1]
     rows = q_ref.shape[0] // devices
     half = rows // 2
     for j in range(LATENT_BLOCKS):
@@ -91,8 +104,8 @@
     for i in range(places // TILE):
         scores = lax.dot_general(
             q_ref[...],
-            cache_ref[i * TILE : (i + 1) * TILE, :],
-            (((1,), (1,)), ((), ())),
+            cache_ref[:, i * TILE : (i + 1) * TILE],
+            (((1,), (0,)), ((), ())),
             preferred_element_type=F32,
         )
         scores = jnp.where(limits >= i * TILE, scores, negative)
@@ -107,7 +120,13 @@
             total += weights[:, j * LANES : (j + 1) * LANES]
         p_ref[:, i * TILE : (i + 1) * TILE] = weights.astype(BF16)
     total = jnp.sum(total, axis=1, keepdims=True)
-    share = jnp.dot(p_ref[...], cache_ref[:, :LATENT], preferred_element_type=F32) / total
+    share = lax.dot_general(
+        p_ref[...],
+        cache_ref[:LATENT, :],
+        (((1,), (1,)), ((), ())),
+        preferred_element_type=F32,
+    )
+    share = share / total
     for j in range(LATENT_BLOCKS):
         block = share[:, j * LANES : (j + 1) * LANES].astype(BF16)
         sent_ref[:, j * rows : (j + 1) * rows, :] = block.reshape(devices, rows, LANES)
@@ -155,6 +174,27 @@
         sent_ref[d] = values
 
 
+def project_kernel(values_ref, w_out_ref, sent_ref):
+    devices = values_ref.shape[0]
+    blocks = sent_ref.shape[1]
+    values = jnp.concatenate([values_ref[d].astype(F32) for d in range(devices)], axis=0)
+    mixed = jnp.dot(values.astype(BF16), w_out_ref[...], preferred_element_type=F32)
+    width = mixed.shape[1]
+    pad = blocks * LANES - width
+    mixed = jnp.concatenate([mixed, jnp.zeros((mixed.shape[0], pad), F32)], axis=1)
+    sent_ref[...] = mixed.reshape(mixed.shape[0], blocks, LANES).astype(BF16)
+
+
+def total_kernel(arrived_ref, mixed_ref):
+    total = jnp.sum(arrived_ref[...].astype(F32), axis=0)
+    for j in range(mixed_ref.shape[1] // LANES):
+        mixed_ref[:, j * LANES : (j + 1) * LANES] = total[j : j + 1].astype(BF16)
+
+
+def limited(mebibytes):
+    return pltpu.CompilerParams(vmem_limit_bytes=mebibytes * 1024 * 1024)
+
+
 def per_device(queries, cache, lengths, offsets, w_uv, w_out):
     heads = queries.shape[2]
     rows = DRAFT * heads
@@ -168,6 +208,7 @@
         out_shape=jax.ShapeDtypeStruct((devices_ctx, message, LANES), BF16),
         in_specs=[VMEM],
         out_specs=VMEM,
+        compiler_params=limited(4),
         name="pack",
     )(queries)
     arrived = lax.all_to_all(sent, "ctx", 0, 0, tiled=True)
@@ -183,22 +224,38 @@
             pltpu.VMEM((all_rows, places), F32),
             pltpu.VMEM((all_rows, places), BF16),
         ],
-        compiler_params=pltpu.CompilerParams(vmem_limit_bytes=24 * 1024 * 1024),
+        compiler_params=limited(24),
         name="attend",
-    )(scalars, rotation_tables(positions, rows), arrived, cache[0])
+    )(scalars, rotation_tables(positions, rows), arrived, cache[0].T)
     arrived = lax.all_to_all(sent, "ctx", 0, 0, tiled=True)
     sent = pl.pallas_call(
         combine_kernel,
         out_shape=jax.ShapeDtypeStruct((devices_seq, DRAFT, heads * w_uv.shape[2]), BF16),
         in_specs=[VMEM, VMEM],
         out_specs=VMEM,
+        compiler_params=limited(8),
         name="combine",
     )(arrived, w_uv)
     every_token = lax.all_to_all(sent, "seq", 0, 0, tiled=True)
-    every_token = every_token.reshape(devices_seq * DRAFT, w_out.shape[0])
-    mixed = jnp.dot(every_token, w_out, preferred_element_type=F32).astype(BF16)
-    mixed = lax.all_to_all(mixed[:, None, :], ("ctx", "head"), 0, 0, tiled=True)
-    return mixed.astype(F32).sum(axis=0).astype(BF16)
+    width = w_out.shape[1]
+    blocks = -(-width // (LANES * 8)) * 8
+    sent = pl.pallas_call(
+        project_kernel,
+        out_shape=jax.ShapeDtypeStruct((devices_seq * DRAFT, blocks, LANES), BF16),
+        in_specs=[VMEM, VMEM],
+        out_specs=VMEM,
+        compiler_params=limited(8),
+        name="project",
+    )(every_token, w_out)
+    arrived = lax.all_to_all(sent, ("ctx", "head"), 0, 0, tiled=True)
+    return pl.pallas_call(
+        total_kernel,
+        out_shape=jax.ShapeDtypeStruct((1, width), BF16),
+        in_specs=[VMEM],
+        out_specs=VMEM,
+        compiler_params=limited(4),
+        name="total",
+    )(arrived)
 
 
 def solution(mesh):

time: 137 us -> 132 us (0.964)
  local copies, waits for them, and re-layouts: 9.85 us -> 0.98 us
  waiting for transfers between devices: 11.4 us -> 16.3 us
    unnamed x11 -> x8, local copies, waits for them, and re-layouts: 8.48 us -> 0.74 us
    all_to_all x1, waiting for transfers between devices: 11.4 us -> 16.3 us  [per_device(): arrived = lax.all_to_all(sent, 'ctx', 0, 0, tiled=True)]
    pallas_call x1, Pallas kernels: 2.45 us -> 0.69 us  [per_device(): pl.pallas_call(combine_kernel, out_shape=jax.ShapeDtypeStruct((devices_se...]
  transfers between devices with their start and end apart: 1 -> 1, of which waited for: 1 -> 1; matrix products, arithmetic and copies ran while one was open for 5% -> 2% of each run, Pallas kernels for 0% -> 0%
where the time goes in v3:
time: 132 us; the launch traced here: 131 us
  blocking collectives  61 us (46%)
  starting transfers between devices  43.7 us (33%)
  waiting for transfers between devices  16.3 us (12%)
  Pallas kernels  6.38 us (5%)
  other arithmetic  2.17 us (2%)
    all_to_all x1, starting transfers between devices, per_device(): arrived = lax.all_to_all(sent, 'ctx', 0, 0, tiled=True)  43.7 us
    all_to_all x1, blocking collectives, per_device(): arrived = lax.all_to_all(sent, 'ctx', 0, 0, tiled=True)  25.3 us
    all_to_all x1, blocking collectives, per_device(): arrived = lax.all_to_all(sent, ('ctx', 'head'), 0, 0, tiled=True)  20.5 us
    all_to_all x1, waiting for transfers between devices, per_device(): arrived = lax.all_to_all(sent, 'ctx', 0, 0, tiled=True)  16.3 us
    all_to_all x1, blocking collectives, per_device(): every_token = lax.all_to_all(sent, 'seq', 0, 0, tiled=True)  15.1 us
    pallas_call x1, Pallas kernels, per_device(): pl.pallas_call(attend_kernel, out_shape=jax.ShapeDtypeStruct((devices_ctx...  3.98 us
  transfers between devices with their start and end apart: 1, of which 1 were waited for; matrix products, arithmetic and copies ran while one was open for 2% of the time, Pallas kernels for 0%

profile of v3, /device:TPU:80, one launch (start us, length us, event | category | flops | bytes accessed | tf_op | source)
XLA Modules:
  0.0 131.2 jit_solution(15905148850369089996)
XLA Ops:
  0.0 0.0 copy-start.3
  0.0 0.7 copy-done.3
  0.7 0.8 pack.1
  1.5 43.7 %all-to-all-start = ((bf16[16,72,128]{2,1,0:T(8,128)(2,1)}), bf16[16,72,128]{2,1,0:T(8,128)(2,1)}, u32[]{:S(2)}, u32[]{:S(2)}) async-start(bf16[16,72,128]{2,1,0:T(8,128)(2,1)} %pack.1), calls=%async_computation | async-start | bytes 589824 | tf_op jit(solution)/shard_map/all_to_all | solution.py:214
  45.9 0.7 convert_reduce_fusion
  46.5 0.7 subtract_bitcast_fusion.scalars_ref
  47.2 0.1 convert_element_type.8
  47.3 0.1 broadcast_in_dim.6
  47.4 0.1 broadcast_in_dim.7
  47.4 0.7 broadcast_multiply_fusion
  48.2 0.1 fusion
  48.3 0.0 copy-start
  48.3 16.3 %all-to-all-done.arrived_ref = bf16[16,72,128]{2,1,0:T(8,128)(2,1)} async-done(((bf16[16,72,128]{2,1,0:T(8,128)(2,1)}), bf16[16,72,128]{2,1,0:T(8,128)(2,1)}, u32[]{:S(2)}, u32[]{:S(2)}) %all-to-all-start) | async-done | bytes 294944 | tf_op jit(solution)/shard_map/all_to_all | solution.py:214
  64.6 0.0 copy-start.2
  64.6 0.0 copy-start.1
  64.6 0.0 copy-done
  64.6 4.0 %attend.1 = bf16[16,72,128]{2,1,0:T(8,128)(2,1)S(1)} custom-call(s32[4]{0:T(128)S(1)} %subtract_bitcast_fusion.scalars_ref, f32[2,8,128]{2,1,0:T(8,128)S(1)} %tables.1.tables_ref, bf16[16,72,128]{2,1,0:T(8,128)(2,1)} %all-to-all-done.arrived_ref, bf16[576,3072]{1,0:T(8,128)(2,1)S(1)} %bitcast.10), custom_call_target="tpu_custom_call" | custom-call | tf_op jit(solution)/shard_map/attend/pallas_call | solution.py:217
  68.6 25.3 %all_to_all.20.arrived_ref = bf16[16,72,128]{2,1,0:T(8,128)(2,1)S(1)} all-to-all(bf16[16,72,128]{2,1,0:T(8,128)(2,1)S(1)} %attend.1), channel_id=1, replica_groups=mesh['groups'=2,'ctx'=16,'seq'=8,'head'=2] {'ctx'}, dimensions={0} | all-to-all | bytes 589824 | tf_op jit(solution)/shard_map/all_to_all | solution.py:230
  94.0 0.0 copy-done.2
  94.0 0.7 combine.1
  94.6 15.1 %all_to_all.21.values_ref = bf16[8,4,512]{2,1,0:T(4,128)(2,1)S(1)} all-to-all(bf16[8,4,512]{2,1,0:T(4,128)(2,1)S(1)} %combine.1), channel_id=1, replica_groups=mesh['groups'=2,'ctx'=16,'seq'=8,'head'=2] {'seq'}, dimensions={0} | all-to-all | bytes 65536 | tf_op jit(solution)/shard_map/all_to_all | solution.py:239
  109.8 0.0 copy-done.1
  109.8 0.3 project.1
  110.1 20.5 %all_to_all.22.arrived_ref = bf16[32,8,128]{2,1,0:T(8,128)(2,1)S(1)} all-to-all(bf16[32,8,128]{2,1,0:T(8,128)(2,1)S(1)} %project.1), channel_id=1, replica_groups=mesh['groups'=2,'ctx'=16,'seq'=8,'head'=2] {'ctx','head'}, dimensions={0} | all-to-all | bytes 131072 | tf_op jit(solution)/shard_map/all_to_all | solution.py:250
  130.6 0.6 total.1
  (2 shorter events, 0.0 us)
Async XLA Ops:
  0.0 0.7 copy-start.3
  1.5 63.1 %all-to-all-start = ((bf16[16,72,128]{2,1,0:T(8,128)(2,1)}), bf16[16,72,128]{2,1,0:T(8,128)(2,1)}, u32[]{:S(2)}, u32[]{:S(2)}) async-start(bf16[16,72,128]{2,1,0:T(8,128)(2,1)} %pack.1), calls=%async_computation | async-start | bytes 589824 | tf_op jit(solution)/shard_map/all_to_all | solution.py:214
  48.3 16.3 %copy-start = (bf16[1,3072,576]{1,2,0:T(8,128)(2,1)S(1)}, bf16[1,3072,576]{1,2,0:T(8,128)(2,1)}, u32[]{:S(2)}) copy-start(bf16[1,3072,576]{1,2,0:T(8,128)(2,1)} %param.8) | copy-start | bytes 10616836
  64.6 29.3 %copy-start.2 = (bf16[4,512,128]{2,1,0:T(8,128)(2,1)S(1)}, bf16[4,512,128]{2,1,0:T(8,128)(2,1)}, u32[]{:S(2)}) copy-start(bf16[4,512,128]{2,1,0:T(8,128)(2,1)} %w_uv_ref.1) | copy-start | bytes 1572868
  64.6 45.2 %copy-start.1 = (bf16[512,896]{1,0:T(8,128)(2,1)S(1)}, bf16[512,896]{1,0:T(8,128)(2,1)}, u32[]{:S(2)}) copy-start(bf16[512,896]{1,0:T(8,128)(2,1)} %w_out_ref.1) | copy-start | bytes 2752516

commit v4 on v3

--- a/solution.py
+++ b/solution.py
@@ -16,6 +16,7 @@
 LANES = 128
 TILE = 256
 COVER = 1 << 24
+STAGGER = 1000
 
 theta = 10000.0
 negative = -1e30
@@ -50,7 +51,13 @@
     )(jnp.cos(angles), jnp.sin(angles))
 
 
-def pack_kernel(queries_ref, sent_ref):
+def pack_kernel(queries_ref, sent_ref, spun_ref):
+    @pl.when(lax.axis_index("head") == 0)
+    def _():
+        spun_ref[...] = lax.fori_loop(
+            0, STAGGER, lambda i, x: x * 0.999 + 0.5, jnp.ones(spun_ref.shape, F32)
+        )
+
     rows = jnp.concatenate([queries_ref[0, t].astype(F32) for t in range(DRAFT)], axis=0)
     half = rows.shape[0] // 2
     parts = [rows[:, j * LANES : (j + 1) * LANES] for j in range(LATENT_BLOCKS)]
@@ -203,11 +210,14 @@
     devices_seq = lax.axis_size("seq")
     message = LATENT_BLOCKS * rows + rows // 2
     positions = lengths[0] - DRAFT + offsets[0]
-    sent = pl.pallas_call(
+    sent, _ = pl.pallas_call(
         pack_kernel,
-        out_shape=jax.ShapeDtypeStruct((devices_ctx, message, LANES), BF16),
+        out_shape=[
+            jax.ShapeDtypeStruct((devices_ctx, message, LANES), BF16),
+            jax.ShapeDtypeStruct((8, LANES), F32),
+        ],
         in_specs=[VMEM],
-        out_specs=VMEM,
+        out_specs=[VMEM, VMEM],
         compiler_params=limited(4),
         name="pack",
     )(queries)

time: 132 us -> 127 us (0.962)
  blocking collectives: 61 us -> 54.2 us
  Pallas kernels: 6.38 us -> 11.6 us
  waiting for transfers between devices: 16.3 us -> 13.3 us
    all_to_all x1, blocking collectives: 25.3 us -> 18.2 us  [per_device(): arrived = lax.all_to_all(sent, 'ctx', 0, 0, tiled=True)]
    pallas_call x1, Pallas kernels: 0.79 us -> 6.03 us  [per_device(): pl.pallas_call(pack_kernel, out_shape=[jax.ShapeDtypeStruct((devices_ctx,...]
    all_to_all x1, waiting for transfers between devices: 16.3 us -> 13.3 us  [per_device(): arrived = lax.all_to_all(sent, 'ctx', 0, 0, tiled=True)]
where the time goes in v4:
time: 127 us
  blocking collectives  54.2 us (43%)
  starting transfers between devices  43.7 us (34%)
  waiting for transfers between devices  13.3 us (10%)
  Pallas kernels  11.6 us (9%)
  other arithmetic  2.17 us (2%)
    all_to_all x1, starting transfers between devices, per_device(): arrived = lax.all_to_all(sent, 'ctx', 0, 0, tiled=True)  43.7 us
    all_to_all x1, blocking collectives, per_device(): arrived = lax.all_to_all(sent, ('ctx', 'head'), 0, 0, tiled=True)  21 us
    all_to_all x1, blocking collectives, per_device(): arrived = lax.all_to_all(sent, 'ctx', 0, 0, tiled=True)  18.2 us
    all_to_all x1, blocking collectives, per_device(): every_token = lax.all_to_all(sent, 'seq', 0, 0, tiled=True)  15.1 us
    all_to_all x1, waiting for transfers between devices, per_device(): arrived = lax.all_to_all(sent, 'ctx', 0, 0, tiled=True)  13.3 us
    pallas_call x1, Pallas kernels, per_device(): pl.pallas_call(pack_kernel, out_shape=[jax.ShapeDtypeStruct((devices_ctx,...  6.03 us
    pallas_call x1, Pallas kernels, per_device(): pl.pallas_call(attend_kernel, out_shape=jax.ShapeDtypeStruct((devices_ctx...  3.98 us
  transfers between devices with their start and end apart: 1, of which 1 were waited for; matrix products, arithmetic and copies ran while one was open for 2% of the time, Pallas kernels for 0%

profile of v4, /device:TPU:80, one launch (start us, length us, event | category | flops | bytes accessed | tf_op | source)
XLA Modules:
  0.0 126.7 jit_solution(816573896693764720)
XLA Ops:
  0.0 0.0 copy-start.3
  0.0 0.7 copy-done.3
  0.7 6.0 %pack.1 = (bf16[16,72,128]{2,1,0:T(8,128)(2,1)}, f32[8,128]{1,0:T(8,128)}) custom-call(bf16[1,4,4,576]{3,2,1,0:T(4,128)(2,1)S(1)} %copy-done.3), custom_call_target="tpu_custom_call" | custom-call | tf_op jit(solution)/shard_map/pack/pallas_call | solution.py:213
  6.8 43.7 %all-to-all-start = ((bf16[16,72,128]{2,1,0:T(8,128)(2,1)}), bf16[16,72,128]{2,1,0:T(8,128)(2,1)}, u32[]{:S(2)}, u32[]{:S(2)}) async-start(bf16[16,72,128]{2,1,0:T(8,128)(2,1)} %get-tuple-element.6), calls=%async_computation | async-start | bytes 589824 | tf_op jit(solution)/shard_map/all_to_all | solution.py:224
  51.1 0.7 convert_reduce_fusion
  51.8 0.7 subtract_bitcast_fusion.scalars_ref
  52.4 0.1 convert_element_type.8
  52.5 0.1 broadcast_in_dim.6
  52.6 0.1 broadcast_in_dim.7
  52.7 0.7 broadcast_multiply_fusion
  53.4 0.1 fusion
  53.5 0.0 copy-start
  53.6 13.3 %all-to-all-done.arrived_ref = bf16[16,72,128]{2,1,0:T(8,128)(2,1)} async-done(((bf16[16,72,128]{2,1,0:T(8,128)(2,1)}), bf16[16,72,128]{2,1,0:T(8,128)(2,1)}, u32[]{:S(2)}, u32[]{:S(2)}) %all-to-all-start) | async-done | bytes 294944 | tf_op jit(solution)/shard_map/all_to_all | solution.py:224
  66.8 0.0 copy-start.2
  66.8 0.0 copy-start.1
  66.8 0.0 copy-done
  66.8 4.0 %attend.1 = bf16[16,72,128]{2,1,0:T(8,128)(2,1)S(1)} custom-call(s32[4]{0:T(128)S(1)} %subtract_bitcast_fusion.scalars_ref, f32[2,8,128]{2,1,0:T(8,128)S(1)} %tables.1.tables_ref, bf16[16,72,128]{2,1,0:T(8,128)(2,1)} %all-to-all-done.arrived_ref, bf16[576,3072]{1,0:T(8,128)(2,1)S(1)} %bitcast.10), custom_call_target="tpu_custom_call" | custom-call | tf_op jit(solution)/shard_map/attend/pallas_call | solution.py:227
  70.8 18.2 %all_to_all.20.arrived_ref = bf16[16,72,128]{2,1,0:T(8,128)(2,1)S(1)} all-to-all(bf16[16,72,128]{2,1,0:T(8,128)(2,1)S(1)} %attend.1), channel_id=1, replica_groups=mesh['groups'=2,'ctx'=16,'seq'=8,'head'=2] {'ctx'}, dimensions={0} | all-to-all | bytes 589824 | tf_op jit(solution)/shard_map/all_to_all | solution.py:240
  89.1 0.0 copy-done.2
  89.1 0.7 combine.1
  89.8 15.1 %all_to_all.21.values_ref = bf16[8,4,512]{2,1,0:T(4,128)(2,1)S(1)} all-to-all(bf16[8,4,512]{2,1,0:T(4,128)(2,1)S(1)} %combine.1), channel_id=1, replica_groups=mesh['groups'=2,'ctx'=16,'seq'=8,'head'=2] {'seq'}, dimensions={0} | all-to-all | bytes 65536 | tf_op jit(solution)/shard_map/all_to_all | solution.py:249
  104.8 0.0 copy-done.1
  104.8 0.3 project.1
  105.1 21.0 %all_to_all.22.arrived_ref = bf16[32,8,128]{2,1,0:T(8,128)(2,1)S(1)} all-to-all(bf16[32,8,128]{2,1,0:T(8,128)(2,1)S(1)} %project.1), channel_id=1, replica_groups=mesh['groups'=2,'ctx'=16,'seq'=8,'head'=2] {'ctx','head'}, dimensions={0} | all-to-all | bytes 131072 | tf_op jit(solution)/shard_map/all_to_all | solution.py:260
  126.1 0.6 total.1
  (2 shorter events, 0.0 us)
Async XLA Ops:
  0.0 0.7 copy-start.3
  6.8 60.1 %all-to-all-start = ((bf16[16,72,128]{2,1,0:T(8,128)(2,1)}), bf16[16,72,128]{2,1,0:T(8,128)(2,1)}, u32[]{:S(2)}, u32[]{:S(2)}) async-start(bf16[16,72,128]{2,1,0:T(8,128)(2,1)} %get-tuple-element.6), calls=%async_computation | async-start | bytes 589824 | tf_op jit(solution)/shard_map/all_to_all | solution.py:224
  53.5 13.3 %copy-start = (bf16[1,3072,576]{1,2,0:T(8,128)(2,1)S(1)}, bf16[1,3072,576]{1,2,0:T(8,128)(2,1)}, u32[]{:S(2)}) copy-start(bf16[1,3072,576]{1,2,0:T(8,128)(2,1)} %param.8) | copy-start | bytes 10616836
  66.8 22.2 %copy-start.2 = (bf16[4,512,128]{2,1,0:T(8,128)(2,1)S(1)}, bf16[4,512,128]{2,1,0:T(8,128)(2,1)}, u32[]{:S(2)}) copy-start(bf16[4,512,128]{2,1,0:T(8,128)(2,1)} %w_uv_ref.1) | copy-start | bytes 1572868
  66.8 38.0 %copy-start.1 = (bf16[512,896]{1,0:T(8,128)(2,1)S(1)}, bf16[512,896]{1,0:T(8,128)(2,1)}, u32[]{:S(2)}) copy-start(bf16[512,896]{1,0:T(8,128)(2,1)} %w_out_ref.1) | copy-start | bytes 2752516

commit v5 on v4

--- a/solution.py
+++ b/solution.py
@@ -15,7 +15,7 @@
 DRAFT = 4
 LANES = 128
 TILE = 256
-COVER = 1 << 24
+CHUNK = 512
 STAGGER = 1000
 
 theta = 10000.0
@@ -46,7 +46,6 @@
         in_specs=[VMEM, VMEM],
         out_specs=VMEM,
         compiler_params=limited(4),
-        cost_estimate=pl.CostEstimate(flops=COVER * 1000, bytes_accessed=COVER, transcendentals=0),
         name="tables",
     )(jnp.cos(angles), jnp.sin(angles))
 
@@ -81,11 +80,16 @@
     return first, second, third
 
 
-def attend_kernel(scalars_ref, tables_ref, arrived_ref, cache_ref, sent_ref, q_ref, s_ref, p_ref):
+def attend_kernel(scalars_ref, tables_ref, arrived_ref, cache_ref, sent_ref, q_ref, s_ref, p_ref, held_ref, sems):
     devices = arrived_ref.shape[0]
     places = cache_ref.shape[1]
     rows = q_ref.shape[0] // devices
     half = rows // 2
+    copies = []
+    for i in range(places // CHUNK):
+        at = (slice(None), pl.ds(i * CHUNK, CHUNK))
+        copies.append(pltpu.make_async_copy(cache_ref.at[at], held_ref.at[at], sems.at[i]))
+        copies[i].start()
     for j in range(LATENT_BLOCKS):
         block = arrived_ref[:, j * rows : (j + 1) * rows, :]
         q_ref[:, j * LANES : (j + 1) * LANES] = block.reshape(devices * rows, LANES)
@@ -109,9 +113,11 @@
     limits = limits - lax.broadcasted_iota(jnp.int32, row.shape, 1)
     top = jnp.full((devices * rows, LANES), negative, F32)
     for i in range(places // TILE):
+        if i * TILE % CHUNK == 0:
+            copies[i * TILE // CHUNK].wait()
         scores = lax.dot_general(
             q_ref[...],
-            cache_ref[:, i * TILE : (i + 1) * TILE],
+            held_ref[:, i * TILE : (i + 1) * TILE],
             (((1,), (0,)), ((), ())),
             preferred_element_type=F32,
         )
@@ -129,7 +135,7 @@
     total = jnp.sum(total, axis=1, keepdims=True)
     share = lax.dot_general(
         p_ref[...],
-        cache_ref[:LATENT, :],
+        held_ref[:LATENT, :],
         (((1,), (1,)), ((), ())),
         preferred_element_type=F32,
     )
@@ -227,14 +233,16 @@
     sent = pl.pallas_call(
         attend_kernel,
         out_shape=jax.ShapeDtypeStruct((devices_ctx, message, LANES), BF16),
-        in_specs=[SMEM, VMEM, VMEM, VMEM],
+        in_specs=[SMEM, VMEM, VMEM, pl.BlockSpec(memory_space=pltpu.HBM)],
         out_specs=VMEM,
         scratch_shapes=[
             pltpu.VMEM((all_rows, LATENT + ROPE), BF16),
             pltpu.VMEM((all_rows, places), F32),
             pltpu.VMEM((all_rows, places), BF16),
+            pltpu.VMEM((LATENT + ROPE, places), BF16),
+            pltpu.SemaphoreType.DMA((places // CHUNK,)),
         ],
-        compiler_params=limited(24),
+        compiler_params=limited(52),
         name="attend",
     )(scalars, rotation_tables(positions, rows), arrived, cache[0].T)
     arrived = lax.all_to_all(sent, "ctx", 0, 0, tiled=True)

time: 127 us -> 128 us (level)
  Pallas kernels: 11.6 us -> 12.9 us
where the time goes in v5:
time: 128 us
  blocking collectives  54.2 us (42%)
  starting transfers between devices  43.7 us (34%)
  waiting for transfers between devices  13.2 us (10%)
  Pallas kernels  12.9 us (10%)
  other arithmetic  2.18 us (2%)
    all_to_all x1, starting transfers between devices, per_device(): arrived = lax.all_to_all(sent, 'ctx', 0, 0, tiled=True)  43.7 us
    all_to_all x1, blocking collectives, per_device(): arrived = lax.all_to_all(sent, ('ctx', 'head'), 0, 0, tiled=True)  20.9 us
    all_to_all x1, blocking collectives, per_device(): arrived = lax.all_to_all(sent, 'ctx', 0, 0, tiled=True)  18.2 us
    all_to_all x1, blocking collectives, per_device(): every_token = lax.all_to_all(sent, 'seq', 0, 0, tiled=True)  15.1 us
    all_to_all x1, waiting for transfers between devices, per_device(): arrived = lax.all_to_all(sent, 'ctx', 0, 0, tiled=True)  13.2 us
    pallas_call x1, Pallas kernels, per_device(): pl.pallas_call(pack_kernel, out_shape=[jax.ShapeDtypeStruct((devices_ctx,...  6.04 us
    pallas_call x1, Pallas kernels, per_device(): pl.pallas_call(attend_kernel, out_shape=jax.ShapeDtypeStruct((devices_ctx...  5.25 us
  transfers between devices with their start and end apart: 1, of which 1 were waited for; matrix products, arithmetic and copies ran while one was open for 2% of the time, Pallas kernels for 0%

profile of v5, /device:TPU:80, one launch (start us, length us, event | category | flops | bytes accessed | tf_op | source)
XLA Modules:
  0.0 127.9 jit_solution(15699084077661725894)
XLA Ops:
  0.0 0.0 copy-start.1
  0.0 0.0 copy-start.2
  0.0 0.8 copy-done.2
  0.8 0.0 copy-start
  0.8 6.0 %pack.1 = (bf16[16,72,128]{2,1,0:T(8,128)(2,1)}, f32[8,128]{1,0:T(8,128)}) custom-call(bf16[1,4,4,576]{3,2,1,0:T(4,128)(2,1)S(1)} %copy-done.2), custom_call_target="tpu_custom_call" | custom-call | tf_op jit(solution)/shard_map/pack/pallas_call | solution.py:219
  6.8 43.7 %all-to-all-start = ((bf16[16,72,128]{2,1,0:T(8,128)(2,1)}), bf16[16,72,128]{2,1,0:T(8,128)(2,1)S(1)}, u32[]{:S(2)}, u32[]{:S(2)}) async-start(bf16[16,72,128]{2,1,0:T(8,128)(2,1)} %get-tuple-element.6), calls=%async_computation | async-start | bytes 589824 | tf_op jit(solution)/shard_map/all_to_all | solution.py:230
  51.2 0.7 convert_reduce_fusion
  51.8 0.1 convert_element_type.8
  51.9 0.1 broadcast_in_dim.6
  52.0 0.1 broadcast_in_dim.7
  52.1 0.7 broadcast_multiply_fusion
  52.8 0.1 fusion
  53.0 0.7 subtract_bitcast_fusion.scalars_ref
  53.6 13.2 %all-to-all-done.arrived_ref = bf16[16,72,128]{2,1,0:T(8,128)(2,1)S(1)} async-done(((bf16[16,72,128]{2,1,0:T(8,128)(2,1)}), bf16[16,72,128]{2,1,0:T(8,128)(2,1)S(1)}, u32[]{:S(2)}, u32[]{:S(2)}) %all-to-all-start) | async-done | bytes 294944 | tf_op jit(solution)/shard_map/all_to_all | solution.py:230
  66.8 5.2 %attend.1 = bf16[16,72,128]{2,1,0:T(8,128)(2,1)S(1)} custom-call(s32[4]{0:T(128)S(1)} %subtract_bitcast_fusion.scalars_ref, f32[2,8,128]{2,1,0:T(8,128)S(1)} %tables.1.tables_ref, bf16[16,72,128]{2,1,0:T(8,128)(2,1)S(1)} %all-to-all-done.arrived_ref, bf16[576,3072]{1,0:T(8,128)(2,1)} %bitcast.10), custom_call_target="tpu_custom_call" | custom-call | tf_op jit(solution)/shard_map/attend/pallas_call | solution.py:233
  72.1 18.2 %all_to_all.20.arrived_ref = bf16[16,72,128]{2,1,0:T(8,128)(2,1)S(1)} all-to-all(bf16[16,72,128]{2,1,0:T(8,128)(2,1)S(1)} %attend.1), channel_id=1, replica_groups=mesh['groups'=2,'ctx'=16,'seq'=8,'head'=2] {'ctx'}, dimensions={0} | all-to-all | bytes 589824 | tf_op jit(solution)/shard_map/all_to_all | solution.py:248
  90.3 0.0 copy-done.1
  90.3 0.7 combine.1
  91.0 15.1 %all_to_all.21.values_ref = bf16[8,4,512]{2,1,0:T(4,128)(2,1)S(1)} all-to-all(bf16[8,4,512]{2,1,0:T(4,128)(2,1)S(1)} %combine.1), channel_id=1, replica_groups=mesh['groups'=2,'ctx'=16,'seq'=8,'head'=2] {'seq'}, dimensions={0} | all-to-all | bytes 65536 | tf_op jit(solution)/shard_map/all_to_all | solution.py:257
  106.1 0.0 copy-done
  106.1 0.3 project.1
  106.4 20.9 %all_to_all.22.arrived_ref = bf16[32,8,128]{2,1,0:T(8,128)(2,1)S(1)} all-to-all(bf16[32,8,128]{2,1,0:T(8,128)(2,1)S(1)} %project.1), channel_id=1, replica_groups=mesh['groups'=2,'ctx'=16,'seq'=8,'head'=2] {'ctx','head'}, dimensions={0} | all-to-all | bytes 131072 | tf_op jit(solution)/shard_map/all_to_all | solution.py:268
  127.3 0.6 total.1
  (2 shorter events, 0.0 us)
Async XLA Ops:
  0.0 90.3 %copy-start.1 = (bf16[4,512,128]{2,1,0:T(8,128)(2,1)S(1)}, bf16[4,512,128]{2,1,0:T(8,128)(2,1)}, u32[]{:S(2)}) copy-start(bf16[4,512,128]{2,1,0:T(8,128)(2,1)} %w_uv_ref.1) | copy-start | bytes 1572868
  0.0 0.8 copy-start.2
  0.8 105.3 %copy-start = (bf16[512,896]{1,0:T(8,128)(2,1)S(1)}, bf16[512,896]{1,0:T(8,128)(2,1)}, u32[]{:S(2)}) copy-start(bf16[512,896]{1,0:T(8,128)(2,1)} %w_out_ref.1) | copy-start | bytes 2752516
  6.8 60.0 %all-to-all-start = ((bf16[16,72,128]{2,1,0:T(8,128)(2,1)}), bf16[16,72,128]{2,1,0:T(8,128)(2,1)S(1)}, u32[]{:S(2)}, u32[]{:S(2)}) async-start(bf16[16,72,128]{2,1,0:T(8,128)(2,1)} %get-tuple-element.6), calls=%async_computation | async-start | bytes 589824 | tf_op jit(solution)/shard_map/all_to_all | solution.py:230
